TPU v7x, 256 devices: a whole 4x4x8 slice. The times are simulated.
256 devices in a mesh: dom: 128 (over x, z, y), mp: 2 (over core).
Axes of the slice: x: 4, y: 4, z: 8, core: 2. Of those that a mesh axis runs over, the one named last changes fastest.
Arguments:
- table: bfloat16 [524288, 768], P('dom', 'mp'), may hold values from -6 to 6
- weight_a: bfloat16 [1536, 512], P(None, 'mp'), may hold values from -0.15625 to 0.15625
- bias_a: float32 [512], replicated, may hold values from -3 to 3
- weight_b: bfloat16 [1024, 512], P(None, 'mp'), may hold values from -0.25 to 0.25
- bias_b: float32 [512], replicated, may hold values from -3 to 3
- requests: int32 [128, 128, 16], P('dom'), may hold values from 0 to 4095
- near_a: int32 [131072, 10], P('dom'), may hold values from 0 to 2047
- self_a: int32 [131072], P('dom'), may hold values from 0 to 2047
- count_a: int32 [131072], P('dom'), may hold values from 1 to 10
- near_b: int32 [32768, 5], P('dom'), may hold values from 0 to 1023
- self_b: int32 [32768], P('dom'), may hold values from 0 to 1023
- count_b: int32 [32768], P('dom'), may hold values from 1 to 5
Outputs:
- embedding: bfloat16 [32768, 512], P('dom', 'mp')
Inputs may be any that keep to these rules, and one draw needn't show every extreme that they name: `requests`: local row indices at the owner. `near_a`: slots of the same minibatch; entries at j >= count_a are padding. `near_b`: positions within the same minibatch; entries at j >= count_b are padding.
All inputs are finite; a program needn't handle non-finite values.
Results may differ from a plain program's by a relative error of at most 0.0074.
Values may be sent and summed in bfloat16 or wider, within the bound.
A program may use at most 64 MiB of HBM per device.

v0:
```python
import jax
import jax.numpy as jnp
from jax import lax
from jax.sharding import PartitionSpec as P

F = 768
H = 512


def sent_together(arrays, axis, dim, along):
    widths = [a.shape[along] for a in arrays]
    both = jnp.concatenate(arrays, axis=along)
    result = lax.all_gather(both, axis, axis=dim, tiled=True)
    return tuple(jnp.split(result, [sum(widths[:k]) for k in range(1, len(widths))], axis=along))


def total_of_pieces(shard, axis):
    return lax.all_gather(shard, axis).sum(0)


def from_everyone(shard, axis):
    peers = lax.axis_size(axis)
    return lax.all_to_all(
        jnp.broadcast_to(shard[None], (peers, *shard.shape)), axis, 0, 0, tiled=True
    )


def in_order(pieces, dim):
    dims = list(pieces.shape[1:])
    dims[dim] *= pieces.shape[0]
    return jnp.moveaxis(pieces, 0, dim).reshape(dims)


def gathered_copies(shard, axis, dim):
    pieces = from_everyone(shard, axis)
    return in_order(pieces, dim)


def in_blocks(shard, dim, peers):
    dims = shard.shape
    pieces = shard.reshape(*dims[:dim], peers, dims[dim] // peers, *dims[dim + 1 :])
    return jnp.moveaxis(pieces, dim, 0)


def sum_at_owner(shard, axis, dim):
    peers = lax.axis_size(axis)
    pieces = lax.all_to_all(in_blocks(shard, dim, peers), axis, 0, 0, tiled=True)
    return jnp.sum(pieces.astype(jnp.float32), axis=0)


def mean_rows(source, neighbours, counts):
    total_rows = neighbours.shape[0]
    fanout = neighbours.shape[1]
    block = min(512, total_rows)
    columns = lax.broadcasted_iota(jnp.int32, (1, source.shape[0]), 1)

    def one_block(pieces):
        near, valid = pieces
        weights = jnp.zeros((block, source.shape[0]), jnp.bfloat16)
        for column in range(fanout):
            picked = (near[:, column : column + 1] == columns) & (valid[:, None] > column)
            weights = weights + picked.astype(jnp.bfloat16)
        total = jnp.dot(weights, source, preferred_element_type=jnp.float32)
        return (total / valid[:, None].astype(jnp.float32)).astype(jnp.bfloat16)

    result = lax.map(one_block, (neighbours.reshape(-1, block, fanout), counts.reshape(-1, block)))
    return result.reshape(total_rows, source.shape[1])


def shards(
    table,
    weight_a,
    bias_a,
    weight_b,
    bias_b,
    requests,
    near_a,
    self_a,
    count_a,
    near_b,
    self_b,
    count_b,
):
    half_hidden = weight_a.shape[1]
    half_feature = table.shape[1]
    mp_index = lax.axis_index("mp")
    asked = requests[0]
    found = table[lax.all_to_all(asked, "dom", split_axis=0, concat_axis=0, tiled=True)]
    fetched = lax.all_to_all(found, "dom", split_axis=0, concat_axis=0, tiled=True)
    fetched = fetched.reshape(-1, half_feature)
    own_rows = fetched[self_a]
    mean_a = mean_rows(fetched, near_a, count_a)
    whole_a = gathered_copies(weight_a, "mp", 1)
    own_weight = lax.dynamic_slice_in_dim(whole_a, mp_index * half_feature, half_feature, 0)
    near_weight = lax.dynamic_slice_in_dim(whole_a, F + mp_index * half_feature, half_feature, 0)
    partial_value = jnp.dot(own_rows, own_weight, preferred_element_type=jnp.float32)
    partial_value = partial_value + jnp.dot(mean_a, near_weight, preferred_element_type=jnp.float32)
    bias_part = lax.dynamic_slice_in_dim(bias_a, mp_index * half_hidden, half_hidden, 0)
    before = sum_at_owner(partial_value.astype(jnp.bfloat16), "mp", 1) + bias_part
    hidden_a = jax.nn.relu(before).astype(jnp.bfloat16)
    bias_part = lax.dynamic_slice_in_dim(bias_b, mp_index * half_hidden, half_hidden, 0)
    mean_b = mean_rows(hidden_a, near_b, count_b)
    own_b, mean_whole = sent_together((hidden_a[self_b], mean_b), "mp", 1, 0)
    inputs_b = jnp.concatenate([own_b, mean_whole], axis=1)
    state = jax.nn.relu(jnp.dot(inputs_b, weight_b, preferred_element_type=jnp.float32) + bias_part)
    squares = total_of_pieces(jnp.sum(state * state, axis=1), "mp")
    scaled = state * jnp.sqrt(jnp.float32(H)) / jnp.sqrt(squares[:, None] + H)
    return scaled.astype(jnp.bfloat16)


def solution(mesh):
    placed = (
        P("dom", "mp"),
        P(None, "mp"),
        P(),
        P(None, "mp"),
        P(),
        P("dom", None, None),
        P("dom", None),
        P("dom"),
        P("dom"),
        P("dom", None),
        P("dom"),
        P("dom"),
    )
    return jax.shard_map(
        shards, mesh=mesh, in_specs=placed, out_specs=P("dom", "mp"), check_vma=False
    )
```

profile of v0, /device:TPU:1, one launch (start us, length us, event | category | flops | bytes accessed | tf_op | source)
XLA Modules:
  0.0 146.2 jit_solution(8767340318164387549)
XLA Ops:
  0.0 0.0 copy-start
  0.0 0.9 copy.21
  0.9 26.9 %all_to_all.27 = s32[128,1,16]{2,1,0:T(1,128)S(1)} all-to-all(s32[128,1,16]{2,1,0:T(1,128)S(1)} %bitcast.77), channel_id=1, replica_groups=mesh['dom'=128,'mp'=2] {'dom'}, dimensions={0} | all-to-all | bytes 16384 | tf_op jit(solution)/shard_map/all_to_all | solution.py:88
  27.8 0.1 reshape.186
  27.9 0.0 copy-done
  27.9 9.0 %gather_fusion = bf16[2048,384]{1,0:T(8,128)(2,1)} fusion(bf16[4096,384]{1,0:T(8,128)(2,1)S(1)} %copy-done, s32[2048]{0:T(1024)S(1)} %broadcast_clamp_fusion), kind=kCustom, calls=%fused_computation | custom fusion | bytes 3153920 | tf_op jit(solution)/shard_map/gather | solution.py:88
  36.9 0.0 copy-start.8
  36.9 0.0 copy-start.9
  36.9 0.0 copy-start.3
  36.9 0.0 copy-start.4
  37.0 0.0 copy-start.2
  37.0 0.0 copy-start.7
  37.0 0.0 copy-start.5
  37.0 0.0 copy-start.6
  37.0 7.4 %all-to-all-start.1 = ((bf16[128,16,384]{2,1,0:T(8,128)(2,1)}), bf16[128,16,384]{2,1,0:T(8,128)(2,1)}, u32[]{:S(2)}, u32[]{:S(2)}) async-start(bf16[128,16,384]{2,1,0:T(8,128)(2,1)} %bitcast.72), calls=%async_computation.1 | async-start | bytes 3145728 | tf_op jit(solution)/shard_map/all_to_all | solution.py:89
  44.4 0.0 copy-done.8
  44.4 0.1 dynamic_slice.28
  44.5 0.0 copy-done.9
  44.5 0.1 dynamic_slice.29
  44.6 0.0 copy-done.3
  44.6 0.0 copy-done.4
  44.6 0.0 copy-done.2
  44.7 2.3 %copy.22 = bf16[1536,256]{0,1:T(8,128)(2,1)} copy(bf16[1536,256]{1,0:T(8,128)(2,1)} %param.15) | data formatting | bytes 1572864 | tf_op args[1]
  47.0 0.0 copy-done.7
  47.0 0.0 copy-done.5
  47.1 0.0 copy-done.6
  47.1 34.7 %all-to-all-done.1 = bf16[128,16,384]{2,1,0:T(8,128)(2,1)} async-done(((bf16[128,16,384]{2,1,0:T(8,128)(2,1)}), bf16[128,16,384]{2,1,0:T(8,128)(2,1)}, u32[]{:S(2)}, u32[]{:S(2)}) %all-to-all-start.1) | async-done | bytes 1572896 | tf_op jit(solution)/shard_map/all_to_all | solution.py:89
  81.8 2.4 %broadcast_in_dim.15 = bf16[2,1536,256]{1,2,0:T(8,128)(2,1)} broadcast(bf16[1536,256]{0,1:T(8,128)(2,1)} %copy.22), dimensions={1,2} | broadcast | bytes 2359296 | tf_op jit(solution)/shard_map/broadcast_in_dim | solution.py:24
  84.2 9.0 %all-to-all-start.2 = ((bf16[2,1536,256]{1,2,0:T(8,128)(2,1)}), bf16[2,1536,256]{1,2,0:T(8,128)(2,1)}, u32[]{:S(2)}, u32[]{:S(2)}) async-start(bf16[2,1536,256]{1,2,0:T(8,128)(2,1)} %broadcast_in_dim.15), calls=%async_computation.2 | async-start | bytes 3145728 | tf_op jit(solution)/shard_map/all_to_all | solution.py:23
  93.2 22.4 %while.16 = (s32[]{:T(128)}, bf16[2,512,384]{2,1,0:T(8,128)(2,1)}, s32[2,512,10]{1,0,2:T(2,128)S(1)}, s32[2,512]{1,0:T(2,128)S(1)}, bf16[2048,384]{1,0:T(8,128)(2,1)}, /*index=5*/s32[]{:T(128)}) while((s32[]{:T(128)}, bf16[2,512,384]{2,1,0:T(8,128)(2,1)}, s32[2,512,10]{1,0,2:T(2,128)S(1)}, s32[2,512]{1,0:T(2,128)S(1)}, ...), condition=%wide.region_1.2_spmd.clone.clone, body=%wide.region_0.1_spmd.clone.clone.sunk | while | flops 858134016 | bytes 2130009 | solution.py:66
  93.2 0.1 compare_reduce_fusion.11
  93.3 11.1 %fusion.133 = bf16[2,512,384]{2,1,0:T(8,128)(2,1)} fusion(bf16[2,512,384]{2,1,0:T(8,128)(2,1)} %get-tuple-element.257, s32[]{:T(128)S(6)} %copy.34, bf16[2048,384]{1,0:T(8,128)(2,1)} %get-tuple-element.266, s32[512]{0:T(512)S(1)} %bitcast.79, s32[512]{0:T(512)S(1)} %bitcast.80, s32[512]{0:T(512)S(1)} %bitcast.81, s32[512]{0:T(512)S(1)} %bitcast.82, ...), kind=kOutput, calls=%fused_computation.67.clone.1 | convolution fusion | flops 858128384 | bytes 1993732 | tf_op jit(solution)/shard_map/while/body/eval_jaxpr/dot_general | solution.py:63
  104.4 0.1 compare_reduce_fusion.11
  104.5 11.0 %fusion.133 = bf16[2,512,384]{2,1,0:T(8,128)(2,1)} fusion(bf16[2,512,384]{2,1,0:T(8,128)(2,1)} %get-tuple-element.257, s32[]{:T(128)S(6)} %copy.34, bf16[2048,384]{1,0:T(8,128)(2,1)} %get-tuple-element.266, s32[512]{0:T(512)S(1)} %bitcast.79, s32[512]{0:T(512)S(1)} %bitcast.80, s32[512]{0:T(512)S(1)} %bitcast.81, s32[512]{0:T(512)S(1)} %bitcast.82, ...), kind=kOutput, calls=%fused_computation.67.clone.1 | convolution fusion | flops 858128384 | bytes 1993732 | tf_op jit(solution)/shard_map/while/body/eval_jaxpr/dot_general | solution.py:63
  115.6 6.5 %gather_fusion.1 = bf16[1024,384]{1,0:T(8,128)(2,1)} fusion(bf16[2048,384]{1,0:T(8,128)(2,1)} %bitcast.3, s32[1024]{0:T(1024)S(1)} %fusion.111), kind=kCustom, calls=%fused_computation.1 | custom fusion | bytes 1576960 | tf_op jit(solution)/shard_map/gather | solution.py:91
  122.0 0.0 all-to-all-done.2
  122.1 0.0 copy-start.1
  122.1 2.0 %fusion.109 = f32[1024,512]{0,1:T(8,128)S(1)} fusion(bf16[1024,384]{1,0:T(8,128)(2,1)} %gather_fusion.1, bf16[1536,512]{0,1:T(8,128)(2,1)} %bitcast.5, s32[]{:T(128)S(6)} %select_n.28), kind=kOutput, calls=%fused_computation.121 | convolution fusion | flops 402653184 | bytes 3276804 | tf_op jit(solution)/shard_map/dot_general | solution.py:96
  124.1 0.0 copy-done.1
  124.1 1.8 %add_convert_fusion = bf16[1024,512]{0,1:T(8,128)(2,1)S(1)} fusion(f32[1024,512]{0,1:T(8,128)S(1)} %fusion.109, bf16[1024,384]{1,0:T(8,128)(2,1)S(1)} %bitcast.75, bf16[1536,512]{0,1:T(8,128)(2,1)} %bitcast.5, s32[]{:T(128)S(6)} %select_n.29), kind=kOutput, calls=%fused_computation.82 | convolution fusion | flops 403701760 | bytes 4325380 | tf_op jit(solution)/shard_map/dot_general | solution.py:97
  125.9 4.4 %all_to_all.28 = bf16[2,1024,256]{1,2,0:T(8,128)(2,1)S(1)} all-to-all(bf16[2,1024,256]{1,2,0:T(8,128)(2,1)S(1)} %bitcast.73), channel_id=1, replica_groups=mesh['dom'=128,'mp'=2] {'mp'}, dimensions={0} | all-to-all | bytes 2097152 | tf_op jit(solution)/shard_map/all_to_all | solution.py:47
  130.3 1.2 convert_reduce_fusion
  131.5 2.5 %copy.24 = f32[1024,256]{1,0:T(8,128)} copy(f32[1024,256]{0,1:T(8,128)} %convert_reduce_fusion) | data formatting | bytes 2097152 | tf_op jit(solution)/shard_map/reduce_sum | solution.py:48
  134.1 2.1 %maximum_convert_fusion = bf16[1024,256]{1,0:T(8,128)(2,1)} fusion(f32[1024,256]{1,0:T(8,128)} %copy.24, f32[256]{0:T(256)S(1)} %dynamic_slice.28), kind=kLoop, calls=%fused_computation.92 | loop fusion | flops 786432 | bytes 1573888 | tf_op jit(solution)/shard_map/convert_element_type | solution.py:100
  136.2 2.1 %gather_fusion.2 = bf16[256,256]{1,0:T(8,128)(2,1)S(1)} fusion(bf16[1024,256]{1,0:T(8,128)(2,1)} %maximum_convert_fusion, s32[1024]{0:T(1024)S(1)} %pad_clamp_fusion), kind=kCustom, calls=%fused_computation.2 | custom fusion | bytes 263168 | tf_op jit(solution)/shard_map/gather | solution.py:103
  138.3 0.0 copy-start.10
  138.3 2.6 %fusion.75 = bf16[256,256]{1,0:T(8,128)(2,1)S(1)} fusion(bf16[1024,256]{1,0:T(8,128)(2,1)} %maximum_convert_fusion, s32[256]{0:T(256)S(1)} %bitcast.92, s32[256]{0:T(256)S(1)} %bitcast.93, s32[256]{0:T(256)S(1)} %bitcast.90, s32[256]{0:T(256)S(1)} %bitcast.91, s32[256]{0:T(256)S(1)} %bitcast.89, pred[256]{0:T(512)(128)(4,1)S(1)} %get-tuple-element.172, ...), kind=kOutput, calls=%fused_computation.86 | convolution fusion | flops 140902400 | bytes 662784 | tf_op jit(solution)/shard_map/while/body/eval_jaxpr/dot_general | solution.py:63
  140.9 2.2 %all_gather.9 = bf16[512,512]{1,0:T(8,128)(2,1)S(1)} all-gather(bf16[512,256]{1,0:T(8,128)(2,1)S(1)} %pad_maximum_fusion), channel_id=1, replica_groups=mesh['dom'=128,'mp'=2] {'mp'}, dimensions={1}, use_global_device_ids=true | all-gather | bytes 786432 | tf_op jit(solution)/shard_map/all_gather | solution.py:13
  143.1 0.0 copy-done.10
  143.1 0.4 multiply_reduce_fusion
  143.5 1.8 %all-gather.1 = f32[2,1,256]{2,1,0:T(1,128)S(1)} all-gather(f32[1,1,256]{2,1,0:T(1,128)S(1)} %bitcast.94), channel_id=2, replica_groups=mesh['dom'=128,'mp'=2] {'mp'}, dimensions={0}, use_global_device_ids=true | all-gather | bytes 3072 | tf_op jit(solution)/shard_map/all_gather | solution.py:18
  145.4 0.8 copy.25
  (24 shorter events, 0.3 us)
Async XLA Ops:
  0.0 27.9 %copy-start = (bf16[4096,384]{1,0:T(8,128)(2,1)S(1)}, bf16[4096,384]{1,0:T(8,128)(2,1)}, u32[]{:S(2)}) copy-start(bf16[4096,384]{1,0:T(8,128)(2,1)} %param.14) | copy-start | bytes 9437188
  36.9 7.5 %copy-start.8 = (f32[512]{0:T(512)S(1)}, f32[512]{0:T(512)}, u32[]{:S(2)}) copy-start(f32[512]{0:T(512)} %param.16) | copy-start | bytes 6148
  36.9 7.6 %copy-start.9 = (f32[512]{0:T(512)S(1)}, f32[512]{0:T(512)}, u32[]{:S(2)}) copy-start(f32[512]{0:T(512)} %param.18) | copy-start | bytes 6148
  36.9 7.7 %copy-start.3 = (s32[256]{0:T(256)S(1)}, s32[256]{0:T(256)}, u32[]{:S(2)}) copy-start(s32[256]{0:T(256)} %param.25) | copy-start | bytes 3076
  36.9 7.7 %copy-start.4 = (s32[1024]{0:T(1024)S(1)}, s32[1024]{0:T(1024)}, u32[]{:S(2)}) copy-start(s32[1024]{0:T(1024)} %param.22) | copy-start | bytes 12292
  37.0 7.7 %copy-start.2 = (s32[1024,10]{0,1:T(8,128)S(1)}, s32[1024,10]{0,1:T(8,128)}, u32[]{:S(2)}) copy-start(s32[1024,10]{0,1:T(8,128)} %param.20) | copy-start | bytes 122884
  37.0 10.1 %copy-start.7 = (s32[256]{0:T(256)S(1)}, s32[256]{0:T(256)}, u32[]{:S(2)}) copy-start(s32[256]{0:T(256)} %param.24) | copy-start | bytes 3076
  37.0 10.1 %copy-start.5 = (s32[1024]{0:T(1024)S(1)}, s32[1024]{0:T(1024)}, u32[]{:S(2)}) copy-start(s32[1024]{0:T(1024)} %param.21) | copy-start | bytes 12292
  37.0 10.1 %copy-start.6 = (s32[256,5]{0,1:T(8,128)S(1)}, s32[256,5]{0,1:T(8,128)}, u32[]{:S(2)}) copy-start(s32[256,5]{0,1:T(8,128)} %param.23) | copy-start | bytes 15364
  37.0 44.8 %all-to-all-start.1 = ((bf16[128,16,384]{2,1,0:T(8,128)(2,1)}), bf16[128,16,384]{2,1,0:T(8,128)(2,1)}, u32[]{:S(2)}, u32[]{:S(2)}) async-start(bf16[128,16,384]{2,1,0:T(8,128)(2,1)} %bitcast.72), calls=%async_computation.1 | async-start | bytes 3145728 | tf_op jit(solution)/shard_map/all_to_all | solution.py:89
  84.2 37.9 %all-to-all-start.2 = ((bf16[2,1536,256]{1,2,0:T(8,128)(2,1)}), bf16[2,1536,256]{1,2,0:T(8,128)(2,1)}, u32[]{:S(2)}, u32[]{:S(2)}) async-start(bf16[2,1536,256]{1,2,0:T(8,128)(2,1)} %broadcast_in_dim.15), calls=%async_computation.2 | async-start | bytes 3145728 | tf_op jit(solution)/shard_map/all_to_all | solution.py:23
  122.1 2.0 %copy-start.1 = (bf16[2,512,384]{2,1,0:T(8,128)(2,1)S(1)}, bf16[2,512,384]{2,1,0:T(8,128)(2,1)}, u32[]{:S(2)}) copy-start(bf16[2,512,384]{2,1,0:T(8,128)(2,1)} %get-tuple-element.82) | copy-start | bytes 2359300
  138.3 4.8 %copy-start.10 = (bf16[1024,256]{1,0:T(8,128)(2,1)S(1)}, bf16[1024,256]{1,0:T(8,128)(2,1)}, u32[]{:S(2)}) copy-start(bf16[1024,256]{1,0:T(8,128)(2,1)} %param.17) | copy-start | bytes 1572868
where the time goes:
time: 147 us; the launch traced here: 146 us
  blocking collectives  35.3 us (24%)
  waiting for transfers between devices  34.7 us (24%)
  matrix products  28.8 us (20%)
  local copies, waits for them, and re-layouts  27 us (18%)
  starting transfers between devices  16.4 us (11%)
  other arithmetic  3.65 us (2%)
    all_to_all x1, waiting for transfers between devices, shards(): lax.all_to_all(found, 'dom', split_axis=0, concat_axis=0, tiled=True)  34.7 us
    all_to_all x1, blocking collectives, shards(): lax.all_to_all(asked, 'dom', split_axis=0, concat_axis=0, tiled=True)  26.9 us
    dot_general x3, matrix products, one_block(): total = jnp.dot(weights, source, preferred_element_type=jnp.float32)  24.7 us
    gather x1, local copies, waits for them, and re-layouts, shards(): table[lax.all_to_all(asked, 'dom', split_axis=0, concat_axis=0, tiled=True)]  9.02 us
    all_to_all x1, starting transfers between devices, from_everyone(): lax.all_to_all(jnp.broadcast_to(shard[None], (peers, *shard.shape)), axis...  9.02 us
    all_to_all x1, starting transfers between devices, shards(): lax.all_to_all(found, 'dom', split_axis=0, concat_axis=0, tiled=True)  7.41 us
    gather x1, local copies, waits for them, and re-layouts, shards(): own_rows = fetched[self_a]  6.47 us
    all_to_all x1, blocking collectives, sum_at_owner(): lax.all_to_all(in_blocks(shard, dim, peers), axis, 0, 0, tiled=True)  4.39 us
  transfers between devices with their start and end apart: 2, of which 1 were waited for; matrix products, arithmetic and copies ran while one was open for 21% of the time, Pallas kernels for 0%

commit v1 on v0

v1 whole, which is shorter than its diff:
```python
import functools

import jax
import jax.numpy as jnp
from jax import lax
from jax.experimental import pallas as pl
from jax.experimental.pallas import tpu as pltpu
from jax.sharding import PartitionSpec as P

F = 768
H = 512
FH = 384
HH = 256
NX, NY, NZ = 4, 4, 8
NP = NX * NY
ROWS = 16
HOP = 1024
SLOTS = 2048
SEEDS = 256
NODE = 4096
BLK = 256
NBLK = HOP // BLK
MESH = pl.DeviceIdType.MESH
I32 = jnp.int32
F32 = jnp.float32
BF = jnp.bfloat16


def kernel(
    table, wa, ba, wb, bb, req, near_a, self_a, cnt_a, near_b, self_b, cnt_b,
    out,
    table_v, wa_v, wb_v, req_v, near_v, selfa_v, cnta_v, nearb_v, selfb_v, cntb_v,
    req2, zreq, tz, pick, stag, xbuf, amat, acc, lo_s, w0_s, w1_s, selfc, invc,
    part, psend, precv, bmat, accb, invb,
    lsem, wsem, wrsem, psem, prsem, zsem, zrsem, fsem, frsem, qsem, qrsem,
):
    d = lax.axis_index("dom")
    c = lax.axis_index("mp")
    x, z, y = d // (NZ * NY), (d // NY) % NZ, d % NY
    qme = x * NY + y
    mate = (d, 1 - c)

    def at_plane(m):
        tx = (x + m // NY) % NX
        ty = (y + m % NY) % NY
        return tx, ty, tx * NY + ty

    def dev(tx, tz_, ty):
        return (tx * (NZ * NY) + tz_ * NY + ty, c)

    local = []

    def bring(src, dst):
        cp = pltpu.make_async_copy(src, dst, lsem.at[len(local)])
        cp.start()
        local.append(cp)
        return cp

    c_req = bring(req, req_v)
    c_idx = [bring(near_a, near_v), bring(self_a, selfa_v), bring(cnt_a, cnta_v)]
    c_tab = bring(table, table_v)
    c_idb = [bring(near_b, nearb_v), bring(self_b, selfb_v), bring(cnt_b, cntb_v)]
    mine = pl.multiple_of(c * FH, 128)
    c_w = [
        bring(wa.at[pl.ds(mine, FH)], wa_v.at[c, pl.ds(0, FH)]),
        bring(wa.at[pl.ds(F + mine, FH)], wa_v.at[c, pl.ds(FH, FH)]),
        bring(wb, wb_v.at[c]),
    ]

    barrier = pltpu.get_barrier_semaphore()
    for m in range(1, NP):
        tx, ty, _ = at_plane(m)
        pl.semaphore_signal(barrier, inc=1, device_id=dev(tx, z, ty), device_id_type=MESH)
    for j in range(1, NZ):
        pl.semaphore_signal(barrier, inc=1, device_id=dev(x, (z + j) % NZ, y), device_id_type=MESH)
    pl.semaphore_signal(barrier, inc=1, device_id=mate, device_id_type=MESH)

    c_req.wait()
    r = req_v[...]
    rows2 = jnp.concatenate(
        [
            jnp.concatenate([r[a * 32 + k * 4 : a * 32 + k * 4 + 4, :] for a in range(NX)], axis=0)
            for k in range(NZ)
        ],
        axis=1,
    )
    req2[...] = rows2.reshape(NP, 1, 128)

    for cp in c_idx:
        cp.wait()

    def place(s):
        kk = (((s >> 6) & 7) - z) & 7
        return (kk << 8) | ((s >> 9) << 6) | (s & 63)

    self_t = place(selfa_v[...]).T
    cnt_t = cnta_v[...].T
    for g in range(HOP // 128):
        rows = pl.ds(g * 128, 128)
        cnt = cnt_t[:, g : g + 1]
        selfc[rows, :] = self_t[:, g : g + 1]
        invc[rows, :] = 1.0 / cnt.astype(F32)
        p = place(near_v[rows, :])
        valid = lax.broadcasted_iota(I32, p.shape, 1) < cnt
        one = jnp.left_shift(jnp.ones_like(p), ((p >> 7) & 7) * 4)
        lo_s[rows, :] = p & 127
        w0_s[rows, :] = jnp.where(valid & (p < 1024), one, 0)
        w1_s[rows, :] = jnp.where(valid & (p >= 1024), one, 0)

    pl.semaphore_wait(barrier, NP - 1 + NZ - 1 + 1)

    for m in range(1, NP):
        tx, ty, q = at_plane(m)
        pltpu.make_async_remote_copy(
            src_ref=req2.at[q], dst_ref=zreq.at[0, qme], send_sem=psem, recv_sem=prsem,
            device_id=dev(tx, z, ty), device_id_type=MESH,
        ).start()
    zreq[0, qme] = req2[qme]

    lanes = lax.broadcasted_iota(I32, (16, 128), 1)

    def build(rb, _):
        rows = pl.ds(pl.multiple_of(rb * 16, 16), 16)
        rows_s = pl.ds(pl.multiple_of(HOP + rb * 16, 16), 16)
        lo, w0, w1 = lo_s[rows, :], w0_s[rows, :], w1_s[rows, :]
        a0 = jnp.zeros((16, 128), I32)
        a1 = jnp.zeros((16, 128), I32)
        for j in range(lo.shape[1]):
            hit = lo[:, j : j + 1] == lanes
            a0 = a0 + jnp.where(hit, w0[:, j : j + 1], 0)
            a1 = a1 + jnp.where(hit, w1[:, j : j + 1], 0)
        own = jnp.broadcast_to(selfc[rows, :], (16, 128))
        for t in range(SLOTS // 128):
            word = a0 if t < 8 else a1
            v = jnp.right_shift(word, 4 * (t % 8)) & 15
            cols = pl.ds(t * 128, 128)
            amat[rows, cols] = v.astype(F32).astype(BF)
            amat[rows_s, cols] = jnp.where(own == lanes + t * 128, 1.0, 0.0).astype(BF)
        return 0

    lax.fori_loop(0, HOP // 16, build, 0)

    got = pltpu.make_async_remote_copy(
        src_ref=req2.at[pl.ds(0, NP - 1)], dst_ref=zreq.at[0, pl.ds(0, NP - 1)],
        send_sem=psem, recv_sem=prsem, device_id=mate, device_id_type=MESH,
    )
    got.wait_recv()

    def z_copy(j):
        return pltpu.make_async_remote_copy(
            src_ref=zreq.at[0], dst_ref=zreq.at[(NZ - j) % NZ],
            send_sem=zsem.at[j], recv_sem=zrsem.at[(NZ - j) % NZ],
            device_id=dev(x, (z + j) % NZ, y), device_id_type=MESH,
        )

    for j in (1, 7, 2, 6, 3, 5, 4):
        z_copy(j).start()

    other = pl.multiple_of((1 - c) * FH, 128)
    w_out = []
    for i, (src, dst) in enumerate(
        (
            (wa.at[pl.ds(other, FH)], wa_v.at[c, pl.ds(0, FH)]),
            (wa.at[pl.ds(F + other, FH)], wa_v.at[c, pl.ds(FH, FH)]),
            (wb, wb_v.at[c]),
        )
    ):
        cp = pltpu.make_async_remote_copy(
            src_ref=src, dst_ref=dst, send_sem=wsem.at[i], recv_sem=wrsem.at[i],
            device_id=mate, device_id_type=MESH,
        )
        cp.start()
        w_out.append(cp)

    c_tab.wait()

    def order(i):
        return (i % 2) * ((i + 1) // 2) + (1 - i % 2) * ((NZ - i // 2) % NZ)

    def feature_send(k, m):
        tx, ty, q = at_plane(m)
        kk = (NZ - k) % NZ
        return pltpu.make_async_remote_copy(
            src_ref=stag.at[k * NP + q], dst_ref=xbuf.at[kk * NP + qme],
            send_sem=fsem.at[k], recv_sem=frsem.at[kk],
            device_id=dev(tx, (z + k) % NZ, ty), device_id_type=MESH,
        )

    def gather(k):
        tz[...] = zreq[k].reshape(NP, 128).T
        idx = tz[pl.ds(pl.multiple_of(z * 16, 16), 16), :]
        for q in range(NP):
            want = jnp.broadcast_to(idx[:, q : q + 1], (16, 128))
            for t in range(NODE // 128):
                pick[pl.ds(q * 16, 16), pl.ds(t * 128, 128)] = jnp.where(
                    want == lanes + t * 128, 1.0, 0.0
                ).astype(BF)
        rows = jnp.dot(pick[...], table_v[...], preferred_element_type=F32)
        stag[pl.ds(k * NP, NP)] = rows.astype(BF).reshape(NP, ROWS, FH)

    def serve(i, _):
        k = order(i)

        @pl.when(i > 0)
        def _():
            pltpu.make_async_remote_copy(
                src_ref=zreq.at[0], dst_ref=zreq.at[k], send_sem=zsem.at[0], recv_sem=zrsem.at[k],
                device_id=mate, device_id_type=MESH,
            ).wait_recv()

        gather(k)

        @pl.when(i > 0)
        def _():
            feature_send(k, 0).start()

        for m in range(1, NP):
            feature_send(k, m).start()
        return 0

    lax.fori_loop(0, NZ, serve, 0)
    xbuf[qme] = stag[qme]

    for cp in c_idb:
        cp.wait()
    selfb_t = selfb_v[...].T
    cntb_t = cntb_v[...].T
    for g in range(SEEDS // 128):
        cnt = cntb_t[:, g : g + 1]
        invb[pl.ds(g * 128, 128), :] = 1.0 / cnt.astype(F32)
        nb = nearb_v[pl.ds(g * 128, 128), :]
        nb = jnp.where(lax.broadcasted_iota(I32, nb.shape, 1) < cnt, nb, -1)
        sb = selfb_t[:, g : g + 1]
        for s in range(8):
            for t in range(HOP // 128):
                tot = jnp.zeros((16, 128), F32)
                for j in range(nb.shape[1]):
                    tot = tot + jnp.where(nb[s * 16 : s * 16 + 16, j : j + 1] == lanes + t * 128, 1.0, 0.0)
                bmat[pl.ds(g * 128 + s * 16, 16), pl.ds(t * 128, 128)] = tot.astype(BF)
                hit = sb[s * 16 : s * 16 + 16] == lanes + t * 128
                bmat[pl.ds(SEEDS + g * 128 + s * 16, 16), pl.ds(t * 128, 128)] = jnp.where(
                    hit, 1.0, 0.0
                ).astype(BF)

    def add_up(k, first):
        xk = xbuf[pl.ds(k * NP, NP)].reshape(BLK, FH)

        def rows_of(b, _):
            rows = pl.ds(pl.multiple_of(b * 512, 512), 512)
            cols = pl.ds(pl.multiple_of(k * BLK, BLK), BLK)
            tot = jnp.dot(amat[rows, cols], xk, preferred_element_type=F32)
            if first:
                acc[rows, :] = tot
            else:
                acc[rows, :] += tot
            return 0

        lax.fori_loop(0, SLOTS // 512, rows_of, 0)

    def arrived(k, n):
        pltpu.make_async_remote_copy(
            src_ref=stag.at[pl.ds(0, n)], dst_ref=xbuf.at[pl.ds(k * NP, n)],
            send_sem=fsem.at[0], recv_sem=frsem.at[k], device_id=mate, device_id_type=MESH,
        ).wait_recv()

    arrived(0, NP - 1)
    add_up(0, True)

    def collect(i, _):
        k = order(i)
        arrived(k, NP)
        add_up(k, False)
        return 0

    lax.fori_loop(1, NZ, collect, 0)

    for cp in c_w:
        cp.wait()
    for cp in w_out:
        cp.wait_recv()

    def half_copy(b):
        return pltpu.make_async_remote_copy(
            src_ref=psend.at[b], dst_ref=precv.at[b], send_sem=qsem.at[b], recv_sem=qrsem.at[b],
            device_id=mate, device_id_type=MESH,
        )

    for b in range(NBLK):
        rows = pl.ds(b * BLK, BLK)
        own = acc[pl.ds(HOP + b * BLK, BLK), :].astype(BF)
        mean = (acc[rows, :] * invc[rows, :]).astype(BF)
        both = jnp.concatenate([own, mean], axis=1)
        for h in range(2):
            v = jnp.dot(both, wa_v[h], preferred_element_type=F32)
            part[rows, pl.ds(h * HH, HH)] = v
            psend[b, :, pl.ds(h * HH, HH)] = v.astype(BF)
        half_copy(b).start()

    for b in range(NBLK):
        rows = pl.ds(b * BLK, BLK)
        half_copy(b).wait_recv()
        v = part[rows, :] + precv[b].astype(F32) + ba[...]
        hid = jnp.maximum(v, 0.0).astype(BF)
        tot = jnp.dot(bmat[:, pl.ds(b * BLK, BLK)], hid, preferred_element_type=F32)
        if b == 0:
            accb[...] = tot
        else:
            accb[...] += tot

    own = accb[pl.ds(SEEDS, SEEDS), :].astype(BF)
    mean = (accb[pl.ds(0, SEEDS), :] * invb[...]).astype(BF)
    both = jnp.concatenate([own, mean], axis=1)

    def state_of(h):
        v = jnp.dot(both, wb_v[h], preferred_element_type=F32) + bb[pl.ds(h, 1), :]
        return jnp.maximum(v, 0.0)

    s0 = state_of(c)
    s1 = state_of(1 - c)
    squares = jnp.sum(s0 * s0, axis=1, keepdims=True) + jnp.sum(s1 * s1, axis=1, keepdims=True)
    out[...] = (s0 * jnp.sqrt(jnp.float32(H)) / jnp.sqrt(squares + H)).astype(BF)

    got.wait_send()
    for j in range(1, NZ):
        z_copy(j).wait_send()
    for cp in w_out:
        cp.wait_send()
    for k in range(NZ):
        n = NP - 1 if k == 0 else NP
        pltpu.make_async_remote_copy(
            src_ref=stag.at[pl.ds(k * NP, n)], dst_ref=xbuf.at[pl.ds(0, n)],
            send_sem=fsem.at[k], recv_sem=frsem.at[0], device_id=mate, device_id_type=MESH,
        ).wait_send()
    for b in range(NBLK):
        half_copy(b).wait_send()


def shards(
    table, weight_a, bias_a, weight_b, bias_b, requests,
    near_a, self_a, count_a, near_b, self_b, count_b,
):
    vmem = pl.BlockSpec(memory_space=pltpu.VMEM)
    hbm = pl.BlockSpec(memory_space=pl.ANY)
    dma = pltpu.SemaphoreType.DMA
    return pl.pallas_call(
        kernel,
        name="sage",
        out_shape=jax.ShapeDtypeStruct((SEEDS, HH), BF),
        in_specs=[hbm, hbm, vmem, hbm, vmem] + [hbm] * 7,
        out_specs=vmem,
        scratch_shapes=[
            pltpu.VMEM((NODE, FH), BF),
            pltpu.VMEM((2, 2 * FH, HH), BF),
            pltpu.VMEM((2, 2 * H, HH), BF),
            pltpu.VMEM((128, 16), I32),
            pltpu.VMEM((HOP, 10), I32),
            pltpu.VMEM((HOP // 128, 128), I32),
            pltpu.VMEM((HOP // 128, 128), I32),
            pltpu.VMEM((SEEDS, 5), I32),
            pltpu.VMEM((SEEDS // 128, 128), I32),
            pltpu.VMEM((SEEDS // 128, 128), I32),
            pltpu.VMEM((NP, 1, 128), I32),
            pltpu.VMEM((NZ, NP, 1, 128), I32),
            pltpu.VMEM((128, NP), I32),
            pltpu.VMEM((BLK, NODE), BF),
            pltpu.VMEM((NZ * NP, ROWS, FH), BF),
            pltpu.VMEM((NZ * NP, ROWS, FH), BF),
            pltpu.VMEM((2 * HOP, SLOTS), BF),
            pltpu.VMEM((2 * HOP, FH), F32),
            pltpu.VMEM((HOP, 10), I32),
            pltpu.VMEM((HOP, 10), I32),
            pltpu.VMEM((HOP, 10), I32),
            pltpu.VMEM((HOP, 1), I32),
            pltpu.VMEM((HOP, 1), F32),
            pltpu.VMEM((HOP, H), F32),
            pltpu.VMEM((NBLK, BLK, H), BF),
            pltpu.VMEM((NBLK, BLK, H), BF),
            pltpu.VMEM((2 * SEEDS, HOP), BF),
            pltpu.VMEM((2 * SEEDS, H), F32),
            pltpu.VMEM((SEEDS, 1), F32),
            dma((11,)),
            dma((3,)),
            dma((3,)),
            dma,
            dma,
            dma((NZ,)),
            dma((NZ,)),
            dma((NZ,)),
            dma((NZ,)),
            dma((NBLK,)),
            dma((NBLK,)),
        ],
        compiler_params=pltpu.CompilerParams(
            collective_id=0, has_side_effects=True, vmem_limit_bytes=60 * 1024 * 1024
        ),
    )(
        table,
        weight_a,
        bias_a.reshape(1, H),
        weight_b,
        bias_b.reshape(2, HH),
        requests.reshape(128, 16),
        near_a,
        self_a.reshape(HOP // 128, 128),
        count_a.reshape(HOP // 128, 128),
        near_b,
        self_b.reshape(SEEDS // 128, 128),
        count_b.reshape(SEEDS // 128, 128),
    )


def solution(mesh):
    placed = (
        P("dom", "mp"),
        P(None, "mp"),
        P(),
        P(None, "mp"),
        P(),
        P("dom", None, None),
        P("dom", None),
        P("dom"),
        P("dom"),
        P("dom", None),
        P("dom"),
        P("dom"),
    )
    return jax.shard_map(
        shards, mesh=mesh, in_specs=placed, out_specs=P("dom", "mp"), check_vma=False
    )
```

time: 147 us -> 77.3 us (0.53)
  the two profiles are of different devices: /device:TPU:1 before, /device:TPU:103 now
where the time goes in v1:
time: 77.3 us; the launch traced here: 77 us
  Pallas kernels  69.4 us (90%)
  local copies, waits for them, and re-layouts  7.59 us (10%)
    pallas_call x1, Pallas kernels, shards(): pl.pallas_call(kernel, name='sage', out_shape=jax.ShapeDtypeStruct((SEEDS...  69.4 us
    unnamed x4, local copies, waits for them, and re-layouts  6.32 us

profile of v1, /device:TPU:103, one launch (start us, length us, event | category | flops | bytes accessed | tf_op | source)
XLA Modules:
  0.0 77.0 jit_solution(1859821140042695281)
XLA Ops:
  0.0 1.3 %reshape.22.bb = f32[2,256]{1,0:T(2,128)} reshape(f32[512]{0:T(512)} %param.16) | data formatting | bytes 4096 | tf_op jit(solution)/shard_map/reshape | solution.py:401
  1.3 1.4 %copy.13 = s32[1,128,16]{2,1,0:T(8,128)} copy(s32[1,128,16]{1,2,0:T(8,128)} %param.17) | data formatting | bytes 16384 | tf_op args[5]
  2.7 1.5 %copy.15.near_b = s32[256,5]{1,0:T(8,128)} copy(s32[256,5]{0,1:T(8,128)} %param.21) | data formatting | bytes 10240 | tf_op args[9]
  4.2 1.9 %copy.14.near_a = s32[1024,10]{1,0:T(8,128)} copy(s32[1024,10]{0,1:T(8,128)} %param.18) | data formatting | bytes 81920 | tf_op args[6]
  6.0 69.4 %sage.1 = bf16[256,256]{1,0:T(8,128)(2,1)} custom-call(bf16[4096,384]{1,0:T(8,128)(2,1)} %table.1, bf16[1536,256]{1,0:T(8,128)(2,1)} %wa.1, f32[1,512]{1,0:T(1,128)} %bitcast.9, bf16[1024,256]{1,0:T(8,128)(2,1)} %wb.1, f32[2,256]{1,0:T(2,128)} %reshape.22.bb, s32[128,16]{1,0:T(8,128)} %bitcast.6, s32[1024,10]{1,0:T(8,128)} %copy.14.near_a, ...), custom_call_target="tpu_custom_call" | custom-call | tf_op jit(solution)/shard_map/sage/pallas_call | solution.py:345
  75.4 1.6 %copy.17 = bf16[256,256]{1,0:T(8,128)(2,1)} copy(bf16[256,256]{1,0:T(8,128)(2,1)} %sage.1) | data formatting | bytes 262144

commit v2 on v1

--- a/solution.py
+++ b/solution.py
@@ -18,6 +18,8 @@
 SLOTS = 2048
 SEEDS = 256
 NODE = 4096
+EARLY = 28
+ORDER = (0, 1, 7, 2, 6, 3, 5, 4)
 BLK = 256
 NBLK = HOP // BLK
 MESH = pl.DeviceIdType.MESH
@@ -76,7 +78,7 @@
     pl.semaphore_signal(barrier, inc=1, device_id=mate, device_id_type=MESH)
 
     c_req.wait()
-    r = req_v[...]
+    r = req_v[...].T
     rows2 = jnp.concatenate(
         [
             jnp.concatenate([r[a * 32 + k * 4 : a * 32 + k * 4 + 4, :] for a in range(NX)], axis=0)
@@ -94,18 +96,19 @@
         return (kk << 8) | ((s >> 9) << 6) | (s & 63)
 
     self_t = place(selfa_v[...]).T
-    cnt_t = cnta_v[...].T
+    inv_t = (1.0 / cnta_v[...].astype(F32)).T
+    filler = jnp.zeros((16 - near_v.shape[0], 128), I32)
     for g in range(HOP // 128):
         rows = pl.ds(g * 128, 128)
-        cnt = cnt_t[:, g : g + 1]
         selfc[rows, :] = self_t[:, g : g + 1]
-        invc[rows, :] = 1.0 / cnt.astype(F32)
-        p = place(near_v[rows, :])
-        valid = lax.broadcasted_iota(I32, p.shape, 1) < cnt
+        invc[rows, :] = inv_t[:, g : g + 1]
+        p = place(near_v[:, rows])
+        valid = lax.broadcasted_iota(I32, p.shape, 0) < cnta_v[pl.ds(g, 1), :]
         one = jnp.left_shift(jnp.ones_like(p), ((p >> 7) & 7) * 4)
-        lo_s[rows, :] = p & 127
-        w0_s[rows, :] = jnp.where(valid & (p < 1024), one, 0)
-        w1_s[rows, :] = jnp.where(valid & (p >= 1024), one, 0)
+        w0 = jnp.where(valid & (p < 1024), one, 0)
+        w1 = jnp.where(valid & (p >= 1024), one, 0)
+        for to, v in ((lo_s, p & 127), (w0_s, w0), (w1_s, w1)):
+            to[rows, :] = jnp.concatenate([v, filler], axis=0).T
 
     pl.semaphore_wait(barrier, NP - 1 + NZ - 1 + 1)
 
@@ -125,7 +128,7 @@
         lo, w0, w1 = lo_s[rows, :], w0_s[rows, :], w1_s[rows, :]
         a0 = jnp.zeros((16, 128), I32)
         a1 = jnp.zeros((16, 128), I32)
-        for j in range(lo.shape[1]):
+        for j in range(near_v.shape[0]):
             hit = lo[:, j : j + 1] == lanes
             a0 = a0 + jnp.where(hit, w0[:, j : j + 1], 0)
             a1 = a1 + jnp.where(hit, w1[:, j : j + 1], 0)
@@ -138,7 +141,7 @@
             amat[rows_s, cols] = jnp.where(own == lanes + t * 128, 1.0, 0.0).astype(BF)
         return 0
 
-    lax.fori_loop(0, HOP // 16, build, 0)
+    lax.fori_loop(0, EARLY, build, 0)
 
     got = pltpu.make_async_remote_copy(
         src_ref=req2.at[pl.ds(0, NP - 1)], dst_ref=zreq.at[0, pl.ds(0, NP - 1)],
@@ -175,7 +178,7 @@
     c_tab.wait()
 
     def order(i):
-        return (i % 2) * ((i + 1) // 2) + (1 - i % 2) * ((NZ - i // 2) % NZ)
+        return sum(k * (i == n).astype(I32) for n, k in enumerate(ORDER))
 
     def feature_send(k, m):
         tx, ty, q = at_plane(m)
@@ -219,22 +222,24 @@
         return 0
 
     lax.fori_loop(0, NZ, serve, 0)
+    lax.fori_loop(EARLY, HOP // 16, build, 0)
     xbuf[qme] = stag[qme]
 
     for cp in c_idb:
         cp.wait()
     selfb_t = selfb_v[...].T
-    cntb_t = cntb_v[...].T
+    invb_t = (1.0 / cntb_v[...].astype(F32)).T
     for g in range(SEEDS // 128):
-        cnt = cntb_t[:, g : g + 1]
-        invb[pl.ds(g * 128, 128), :] = 1.0 / cnt.astype(F32)
-        nb = nearb_v[pl.ds(g * 128, 128), :]
-        nb = jnp.where(lax.broadcasted_iota(I32, nb.shape, 1) < cnt, nb, -1)
+        cols = pl.ds(g * 128, 128)
+        invb[cols, :] = invb_t[:, g : g + 1]
+        nb = nearb_v[:, cols]
+        nb = jnp.where(lax.broadcasted_iota(I32, nb.shape, 0) < cntb_v[pl.ds(g, 1), :], nb, -1)
+        nb = jnp.concatenate([nb, jnp.full((8 - nb.shape[0], 128), -1, I32)], axis=0).T
         sb = selfb_t[:, g : g + 1]
         for s in range(8):
             for t in range(HOP // 128):
                 tot = jnp.zeros((16, 128), F32)
-                for j in range(nb.shape[1]):
+                for j in range(nearb_v.shape[0]):
                     tot = tot + jnp.where(nb[s * 16 : s * 16 + 16, j : j + 1] == lanes + t * 128, 1.0, 0.0)
                 bmat[pl.ds(g * 128 + s * 16, 16), pl.ds(t * 128, 128)] = tot.astype(BF)
                 hit = sb[s * 16 : s * 16 + 16] == lanes + t * 128
@@ -267,7 +272,7 @@
     add_up(0, True)
 
     def collect(i, _):
-        k = order(i)
+        k = (NZ - order(i)) % NZ
         arrived(k, NP)
         add_up(k, False)
         return 0
@@ -312,7 +317,7 @@
     both = jnp.concatenate([own, mean], axis=1)
 
     def state_of(h):
-        v = jnp.dot(both, wb_v[h], preferred_element_type=F32) + bb[pl.ds(h, 1), :]
+        v = jnp.dot(both, wb_v[h], preferred_element_type=F32) + bb[:, pl.ds(pl.multiple_of(h * HH, HH), HH)]
         return jnp.maximum(v, 0.0)
 
     s0 = state_of(c)
@@ -352,11 +357,11 @@
             pltpu.VMEM((NODE, FH), BF),
             pltpu.VMEM((2, 2 * FH, HH), BF),
             pltpu.VMEM((2, 2 * H, HH), BF),
-            pltpu.VMEM((128, 16), I32),
-            pltpu.VMEM((HOP, 10), I32),
+            pltpu.VMEM((16, 128), I32),
+            pltpu.VMEM((10, HOP), I32),
             pltpu.VMEM((HOP // 128, 128), I32),
             pltpu.VMEM((HOP // 128, 128), I32),
-            pltpu.VMEM((SEEDS, 5), I32),
+            pltpu.VMEM((5, SEEDS), I32),
             pltpu.VMEM((SEEDS // 128, 128), I32),
             pltpu.VMEM((SEEDS // 128, 128), I32),
             pltpu.VMEM((NP, 1, 128), I32),
@@ -367,9 +372,9 @@
             pltpu.VMEM((NZ * NP, ROWS, FH), BF),
             pltpu.VMEM((2 * HOP, SLOTS), BF),
             pltpu.VMEM((2 * HOP, FH), F32),
-            pltpu.VMEM((HOP, 10), I32),
-            pltpu.VMEM((HOP, 10), I32),
-            pltpu.VMEM((HOP, 10), I32),
+            pltpu.VMEM((HOP, 16), I32),
+            pltpu.VMEM((HOP, 16), I32),
+            pltpu.VMEM((HOP, 16), I32),
             pltpu.VMEM((HOP, 1), I32),
             pltpu.VMEM((HOP, 1), F32),
             pltpu.VMEM((HOP, H), F32),
@@ -398,12 +403,12 @@
         weight_a,
         bias_a.reshape(1, H),
         weight_b,
-        bias_b.reshape(2, HH),
-        requests.reshape(128, 16),
-        near_a,
+        bias_b.reshape(1, H),
+        jnp.swapaxes(requests[0], 0, 1),
+        near_a.T,
         self_a.reshape(HOP // 128, 128),
         count_a.reshape(HOP // 128, 128),
-        near_b,
+        near_b.T,
         self_b.reshape(SEEDS // 128, 128),
         count_b.reshape(SEEDS // 128, 128),
     )

time: 77.3 us -> 65.9 us (0.85)
  the two profiles are of different devices: /device:TPU:103 before, /device:TPU:67 now
where the time goes in v2:
time: 65.9 us; the launch traced here: 65.7 us
  Pallas kernels  64.1 us (97%)
  local copies, waits for them, and re-layouts  1.57 us (2%)
    pallas_call x1, Pallas kernels, shards(): pl.pallas_call(kernel, name='sage', out_shape=jax.ShapeDtypeStruct((SEEDS...  64.1 us
    unnamed x1, local copies, waits for them, and re-layouts  1.57 us

profile of v2, /device:TPU:67, one launch (start us, length us, event | category | flops | bytes accessed | tf_op | source)
XLA Modules:
  0.0 65.7 jit_solution(15791259857655663699)
XLA Ops:
  0.0 64.1 %sage.1 = bf16[256,256]{1,0:T(8,128)(2,1)} custom-call(bf16[4096,384]{1,0:T(8,128)(2,1)} %table.1, bf16[1536,256]{1,0:T(8,128)(2,1)} %wa.1, f32[1,512]{1,0:T(1,128)} %bitcast.16, bf16[1024,256]{1,0:T(8,128)(2,1)} %wb.1, f32[1,512]{1,0:T(1,128)} %bitcast.17, s32[16,128]{1,0:T(8,128)} %bitcast.12, s32[10,1024]{1,0:T(8,128)} %bitcast.11, s32[8,128]{1,0:T(8,128)} %bitcast.14, ...), custom_call_target="tpu_custom_call" | custom-call | tf_op jit(solution)/shard_map/sage/pallas_call | solution.py:350
  64.2 1.6 %copy.14 = bf16[256,256]{1,0:T(8,128)(2,1)} copy(bf16[256,256]{1,0:T(8,128)(2,1)} %sage.1) | data formatting | bytes 262144

commit v3 on v2

--- a/solution.py
+++ b/solution.py
@@ -18,7 +18,6 @@
 SLOTS = 2048
 SEEDS = 256
 NODE = 4096
-EARLY = 28
 ORDER = (0, 1, 7, 2, 6, 3, 5, 4)
 BLK = 256
 NBLK = HOP // BLK
@@ -31,7 +30,7 @@
 def kernel(
     table, wa, ba, wb, bb, req, near_a, self_a, cnt_a, near_b, self_b, cnt_b,
     out,
-    table_v, wa_v, wb_v, req_v, near_v, selfa_v, cnta_v, nearb_v, selfb_v, cntb_v,
+    table_v, wa_v, wb_v, ba_v, bb_v, req_v, near_v, selfa_v, cnta_v, nearb_v, selfb_v, cntb_v,
     req2, zreq, tz, pick, stag, xbuf, amat, acc, lo_s, w0_s, w1_s, selfc, invc,
     part, psend, precv, bmat, accb, invb,
     lsem, wsem, wrsem, psem, prsem, zsem, zrsem, fsem, frsem, qsem, qrsem,
@@ -62,6 +61,7 @@
     c_idx = [bring(near_a, near_v), bring(self_a, selfa_v), bring(cnt_a, cnta_v)]
     c_tab = bring(table, table_v)
     c_idb = [bring(near_b, nearb_v), bring(self_b, selfb_v), bring(cnt_b, cntb_v)]
+    c_bias = [bring(ba, ba_v), bring(bb, bb_v)]
     mine = pl.multiple_of(c * FH, 128)
     c_w = [
         bring(wa.at[pl.ds(mine, FH)], wa_v.at[c, pl.ds(0, FH)]),
@@ -87,6 +87,99 @@
         axis=1,
     )
     req2[...] = rows2.reshape(NP, 1, 128)
+
+    pl.semaphore_wait(barrier, NP - 1 + NZ - 1 + 1)
+
+    for m in range(1, NP):
+        tx, ty, q = at_plane(m)
+        pltpu.make_async_remote_copy(
+            src_ref=req2.at[q], dst_ref=zreq.at[0, qme], send_sem=psem, recv_sem=prsem,
+            device_id=dev(tx, z, ty), device_id_type=MESH,
+        ).start()
+    zreq[0, qme] = req2[qme]
+
+    lanes = lax.broadcasted_iota(I32, (16, 128), 1)
+
+    got = pltpu.make_async_remote_copy(
+        src_ref=req2.at[pl.ds(0, NP - 1)], dst_ref=zreq.at[0, pl.ds(0, NP - 1)],
+        send_sem=psem, recv_sem=prsem, device_id=mate, device_id_type=MESH,
+    )
+    got.wait_recv()
+
+    def z_copy(j):
+        return pltpu.make_async_remote_copy(
+            src_ref=zreq.at[0], dst_ref=zreq.at[(NZ - j) % NZ],
+            send_sem=zsem.at[j], recv_sem=zrsem.at[(NZ - j) % NZ],
+            device_id=dev(x, (z + j) % NZ, y), device_id_type=MESH,
+        )
+
+    for j in (1, 7, 2, 6, 3, 5, 4):
+        z_copy(j).start()
+
+    other = pl.multiple_of((1 - c) * FH, 128)
+    w_out = []
+    for i, (src, dst) in enumerate(
+        (
+            (wa.at[pl.ds(other, FH)], wa_v.at[c, pl.ds(0, FH)]),
+            (wa.at[pl.ds(F + other, FH)], wa_v.at[c, pl.ds(FH, FH)]),
+            (wb, wb_v.at[c]),
+        )
+    ):
+        cp = pltpu.make_async_remote_copy(
+            src_ref=src, dst_ref=dst, send_sem=wsem.at[i], recv_sem=wrsem.at[i],
+            device_id=mate, device_id_type=MESH,
+        )
+        cp.start()
+        w_out.append(cp)
+
+    c_tab.wait()
+
+    def order(i):
+        return sum(k * (i == n).astype(I32) for n, k in enumerate(ORDER))
+
+    def feature_send(k, m):
+        tx, ty, q = at_plane(m)
+        kk = (NZ - k) % NZ
+        return pltpu.make_async_remote_copy(
+            src_ref=stag.at[k * NP + q], dst_ref=xbuf.at[kk * NP + qme],
+            send_sem=fsem.at[k], recv_sem=frsem.at[kk],
+            device_id=dev(tx, (z + k) % NZ, ty), device_id_type=MESH,
+        )
+
+    def gather(k):
+        tz[...] = zreq[k].reshape(NP, 128).T
+        idx = tz[pl.ds(pl.multiple_of(z * 16, 16), 16), :]
+        for q in range(NP):
+            want = jnp.broadcast_to(idx[:, q : q + 1], (16, 128))
+            for t in range(NODE // 128):
+                pick[pl.ds(q * 16, 16), pl.ds(t * 128, 128)] = jnp.where(
+                    want == lanes + t * 128, 1.0, 0.0
+                ).astype(BF)
+        rows = jnp.dot(pick[...], table_v[...], preferred_element_type=F32)
+        stag[pl.ds(k * NP, NP)] = rows.astype(BF).reshape(NP, ROWS, FH)
+
+    def serve(i, _):
+        k = order(i)
+
+        @pl.when(k > 0)
+        def _():
+            pltpu.make_async_remote_copy(
+                src_ref=zreq.at[0], dst_ref=zreq.at[k], send_sem=zsem.at[0], recv_sem=zrsem.at[k],
+                device_id=mate, device_id_type=MESH,
+            ).wait_recv()
+
+        gather(k)
+
+        @pl.when(k > 0)
+        def _():
+            feature_send(k, 0).start()
+
+        for m in range(1, NP):
+            feature_send(k, m).start()
+        return 0
+
+    lax.fori_loop(0, NZ, serve, 0)
+    xbuf[qme] = stag[qme]
 
     for cp in c_idx:
         cp.wait()
@@ -109,18 +202,6 @@
         w1 = jnp.where(valid & (p >= 1024), one, 0)
         for to, v in ((lo_s, p & 127), (w0_s, w0), (w1_s, w1)):
             to[rows, :] = jnp.concatenate([v, filler], axis=0).T
-
-    pl.semaphore_wait(barrier, NP - 1 + NZ - 1 + 1)
-
-    for m in range(1, NP):
-        tx, ty, q = at_plane(m)
-        pltpu.make_async_remote_copy(
-            src_ref=req2.at[q], dst_ref=zreq.at[0, qme], send_sem=psem, recv_sem=prsem,
-            device_id=dev(tx, z, ty), device_id_type=MESH,
-        ).start()
-    zreq[0, qme] = req2[qme]
-
-    lanes = lax.broadcasted_iota(I32, (16, 128), 1)
 
     def build(rb, _):
         rows = pl.ds(pl.multiple_of(rb * 16, 16), 16)
@@ -141,89 +222,7 @@
             amat[rows_s, cols] = jnp.where(own == lanes + t * 128, 1.0, 0.0).astype(BF)
         return 0
 
-    lax.fori_loop(0, EARLY, build, 0)
-
-    got = pltpu.make_async_remote_copy(
-        src_ref=req2.at[pl.ds(0, NP - 1)], dst_ref=zreq.at[0, pl.ds(0, NP - 1)],
-        send_sem=psem, recv_sem=prsem, device_id=mate, device_id_type=MESH,
-    )
-    got.wait_recv()
-
-    def z_copy(j):
-        return pltpu.make_async_remote_copy(
-            src_ref=zreq.at[0], dst_ref=zreq.at[(NZ - j) % NZ],
-            send_sem=zsem.at[j], recv_sem=zrsem.at[(NZ - j) % NZ],
-            device_id=dev(x, (z + j) % NZ, y), device_id_type=MESH,
-        )
-
-    for j in (1, 7, 2, 6, 3, 5, 4):
-        z_copy(j).start()
-
-    other = pl.multiple_of((1 - c) * FH, 128)
-    w_out = []
-    for i, (src, dst) in enumerate(
-        (
-            (wa.at[pl.ds(other, FH)], wa_v.at[c, pl.ds(0, FH)]),
-            (wa.at[pl.ds(F + other, FH)], wa_v.at[c, pl.ds(FH, FH)]),
-            (wb, wb_v.at[c]),
-        )
-    ):
-        cp = pltpu.make_async_remote_copy(
-            src_ref=src, dst_ref=dst, send_sem=wsem.at[i], recv_sem=wrsem.at[i],
-            device_id=mate, device_id_type=MESH,
-        )
-        cp.start()
-        w_out.append(cp)
-
-    c_tab.wait()
-
-    def order(i):
-        return sum(k * (i == n).astype(I32) for n, k in enumerate(ORDER))
-
-    def feature_send(k, m):
-        tx, ty, q = at_plane(m)
-        kk = (NZ - k) % NZ
-        return pltpu.make_async_remote_copy(
-            src_ref=stag.at[k * NP + q], dst_ref=xbuf.at[kk * NP + qme],
-            send_sem=fsem.at[k], recv_sem=frsem.at[kk],
-            device_id=dev(tx, (z + k) % NZ, ty), device_id_type=MESH,
-        )
-
-    def gather(k):
-        tz[...] = zreq[k].reshape(NP, 128).T
-        idx = tz[pl.ds(pl.multiple_of(z * 16, 16), 16), :]
-        for q in range(NP):
-            want = jnp.broadcast_to(idx[:, q : q + 1], (16, 128))
-            for t in range(NODE // 128):
-                pick[pl.ds(q * 16, 16), pl.ds(t * 128, 128)] = jnp.where(
-                    want == lanes + t * 128, 1.0, 0.0
-                ).astype(BF)
-        rows = jnp.dot(pick[...], table_v[...], preferred_element_type=F32)
-        stag[pl.ds(k * NP, NP)] = rows.astype(BF).reshape(NP, ROWS, FH)
-
-    def serve(i, _):
-        k = order(i)
-
-        @pl.when(i > 0)
-        def _():
-            pltpu.make_async_remote_copy(
-                src_ref=zreq.at[0], dst_ref=zreq.at[k], send_sem=zsem.at[0], recv_sem=zrsem.at[k],
-                device_id=mate, device_id_type=MESH,
-            ).wait_recv()
-
-        gather(k)
-
-        @pl.when(i > 0)
-        def _():
-            feature_send(k, 0).start()
-
-        for m in range(1, NP):
-            feature_send(k, m).start()
-        return 0
-
-    lax.fori_loop(0, NZ, serve, 0)
-    lax.fori_loop(EARLY, HOP // 16, build, 0)
-    xbuf[qme] = stag[qme]
+    lax.fori_loop(0, HOP // 16, build, 0)
 
     for cp in c_idb:
         cp.wait()
@@ -268,18 +267,12 @@
             send_sem=fsem.at[0], recv_sem=frsem.at[k], device_id=mate, device_id_type=MESH,
         ).wait_recv()
 
-    arrived(0, NP - 1)
-    add_up(0, True)
-
-    def collect(i, _):
-        k = (NZ - order(i)) % NZ
-        arrived(k, NP)
-        add_up(k, False)
-        return 0
-
-    lax.fori_loop(1, NZ, collect, 0)
-
-    for cp in c_w:
+    for i in range(NZ):
+        k = (NZ - ORDER[i]) % NZ
+        arrived(k, NP if k else NP - 1)
+        add_up(k, i == 0)
+
+    for cp in c_bias + c_w:
         cp.wait()
     for cp in w_out:
         cp.wait_recv()
@@ -304,7 +297,7 @@
     for b in range(NBLK):
         rows = pl.ds(b * BLK, BLK)
         half_copy(b).wait_recv()
-        v = part[rows, :] + precv[b].astype(F32) + ba[...]
+        v = part[rows, :] + precv[b].astype(F32) + ba_v[...]
         hid = jnp.maximum(v, 0.0).astype(BF)
         tot = jnp.dot(bmat[:, pl.ds(b * BLK, BLK)], hid, preferred_element_type=F32)
         if b == 0:
@@ -317,7 +310,7 @@
     both = jnp.concatenate([own, mean], axis=1)
 
     def state_of(h):
-        v = jnp.dot(both, wb_v[h], preferred_element_type=F32) + bb[:, pl.ds(pl.multiple_of(h * HH, HH), HH)]
+        v = jnp.dot(both, wb_v[h], preferred_element_type=F32) + bb_v[:, pl.ds(pl.multiple_of(h * HH, HH), HH)]
         return jnp.maximum(v, 0.0)
 
     s0 = state_of(c)
@@ -351,12 +344,14 @@
         kernel,
         name="sage",
         out_shape=jax.ShapeDtypeStruct((SEEDS, HH), BF),
-        in_specs=[hbm, hbm, vmem, hbm, vmem] + [hbm] * 7,
+        in_specs=[hbm] * 12,
         out_specs=vmem,
         scratch_shapes=[
             pltpu.VMEM((NODE, FH), BF),
             pltpu.VMEM((2, 2 * FH, HH), BF),
             pltpu.VMEM((2, 2 * H, HH), BF),
+            pltpu.VMEM((1, H), F32),
+            pltpu.VMEM((1, H), F32),
             pltpu.VMEM((16, 128), I32),
             pltpu.VMEM((10, HOP), I32),
             pltpu.VMEM((HOP // 128, 128), I32),
@@ -383,7 +378,7 @@
             pltpu.VMEM((2 * SEEDS, HOP), BF),
             pltpu.VMEM((2 * SEEDS, H), F32),
             pltpu.VMEM((SEEDS, 1), F32),
-            dma((11,)),
+            dma((13,)),
             dma((3,)),
             dma((3,)),
             dma,
@@ -396,9 +391,12 @@
             dma((NBLK,)),
         ],
         compiler_params=pltpu.CompilerParams(
-            collective_id=0, has_side_effects=True, vmem_limit_bytes=60 * 1024 * 1024
+            collective_id=0, has_side_effects=True, vmem_limit_bytes=50000 * 1024
         ),
     )(
+        *(
+            pltpu.with_memory_space_constraint(v, pltpu.HBM)
+            for v in (
         table,
         weight_a,
         bias_a.reshape(1, H),
@@ -411,6 +409,8 @@
         near_b.T,
         self_b.reshape(SEEDS // 128, 128),
         count_b.reshape(SEEDS // 128, 128),
+            )
+        )
     )
 
 

time: 65.9 us -> 63 us (0.956)
  the two profiles are of different devices: /device:TPU:67 before, /device:TPU:71 now
where the time goes in v3:
time: 63 us; the launch traced here: 62.9 us
  Pallas kernels  62.3 us (99%)
  local copies, waits for them, and re-layouts  0.66 us (1%)
    pallas_call x1, Pallas kernels, shards(): pl.pallas_call(kernel, name='sage', out_shape=jax.ShapeDtypeStruct((SEEDS...  62.3 us

profile of v3, /device:TPU:71, one launch (start us, length us, event | category | flops | bytes accessed | tf_op | source)
XLA Modules:
  0.0 62.9 jit_solution(291813231535585043)
XLA Ops:
  0.0 62.3 %sage.1 = bf16[256,256]{1,0:T(8,128)(2,1)S(1)} custom-call(bf16[4096,384]{1,0:T(8,128)(2,1)} %table.1, bf16[1536,256]{1,0:T(8,128)(2,1)} %wa.1, f32[1,512]{1,0:T(1,128)} %bitcast.16, bf16[1024,256]{1,0:T(8,128)(2,1)} %wb.1, f32[1,512]{1,0:T(1,128)} %bitcast.17, s32[16,128]{1,0:T(8,128)} %bitcast.12, s32[10,1024]{1,0:T(8,128)} %bitcast.11, ...), custom_call_target="tpu_custom_call" | custom-call | tf_op jit(solution)/shard_map/sage/pallas_call | solution.py:343
  62.3 0.7 %copy.14 = bf16[256,256]{1,0:T(8,128)(2,1)} copy(bf16[256,256]{1,0:T(8,128)(2,1)S(1)} %sage.1) | data formatting | bytes 262144

commit v4 on v3

--- a/solution.py
+++ b/solution.py
@@ -18,7 +18,13 @@
 SLOTS = 2048
 SEEDS = 256
 NODE = 4096
-ORDER = (0, 1, 7, 2, 6, 3, 5, 4)
+OFFSET = (
+    (0, 0), (0, 2), (0, 1), (0, 3), (1, 0), (3, 0), (1, 1), (3, 3),
+    (1, 3), (3, 1), (2, 0), (2, 2), (1, 2), (3, 2), (2, 1), (2, 3),
+)
+BACK = tuple(OFFSET.index(((4 - a) % 4, (4 - b) % 4)) for a, b in OFFSET)
+SERVE = (0, 2, 3, 4, 5, 1, 6, 7, 8, 9, 10, 12, 13, 14, 15, 11)
+PAIRS = (1, 2, 0, 3, 4, 6, 7, 5)
 BLK = 256
 NBLK = HOP // BLK
 MESH = pl.DeviceIdType.MESH
@@ -27,11 +33,15 @@
 BF = jnp.bfloat16
 
 
+def look(values, i):
+    return sum(v * (i == n).astype(I32) for n, v in enumerate(values) if v)
+
+
 def kernel(
     table, wa, ba, wb, bb, req, near_a, self_a, cnt_a, near_b, self_b, cnt_b,
     out,
     table_v, wa_v, wb_v, ba_v, bb_v, req_v, near_v, selfa_v, cnta_v, nearb_v, selfb_v, cntb_v,
-    req2, zreq, tz, pick, stag, xbuf, amat, acc, lo_s, w0_s, w1_s, selfc, invc,
+    req_t, req2, zreq, preq, tz, pick, stag, xbuf, amat, acc, lo_s, w0_s, w1_s, selfc, invc,
     part, psend, precv, bmat, accb, invb,
     lsem, wsem, wrsem, psem, prsem, zsem, zrsem, fsem, frsem, qsem, qrsem,
 ):
@@ -41,9 +51,9 @@
     qme = x * NY + y
     mate = (d, 1 - c)
 
-    def at_plane(m):
-        tx = (x + m // NY) % NX
-        ty = (y + m % NY) % NY
+    def at_plane(n):
+        a, b = OFFSET[n] if isinstance(n, int) else (look([o[0] for o in OFFSET], n), look([o[1] for o in OFFSET], n))
+        tx, ty = (x + a) % NX, (y + b) % NY
         return tx, ty, tx * NY + ty
 
     def dev(tx, tz_, ty):
@@ -78,43 +88,44 @@
     pl.semaphore_signal(barrier, inc=1, device_id=mate, device_id_type=MESH)
 
     c_req.wait()
-    r = req_v[...].T
-    rows2 = jnp.concatenate(
-        [
-            jnp.concatenate([r[a * 32 + k * 4 : a * 32 + k * 4 + 4, :] for a in range(NX)], axis=0)
-            for k in range(NZ)
-        ],
-        axis=1,
-    )
-    req2[...] = rows2.reshape(NP, 1, 128)
+    req_t[...] = req_v[...].T
+    for h in range(2):
+        req2[h] = jnp.concatenate(
+            [
+                req_t[pl.ds((q // NY) * 32 + q % NY, NZ, stride=NY), :]
+                for q in range(h * 8, h * 8 + 8)
+            ],
+            axis=1,
+        ).reshape(NZ, 1, 128)
 
     pl.semaphore_wait(barrier, NP - 1 + NZ - 1 + 1)
 
-    for m in range(1, NP):
-        tx, ty, q = at_plane(m)
+    for j in (4, 3, 5, 2, 6, 1, 7):
         pltpu.make_async_remote_copy(
-            src_ref=req2.at[q], dst_ref=zreq.at[0, qme], send_sem=psem, recv_sem=prsem,
-            device_id=dev(tx, z, ty), device_id_type=MESH,
+            src_ref=req2.at[:, (z + j) % NZ], dst_ref=zreq.at[:, NZ - j], send_sem=zsem, recv_sem=zrsem,
+            device_id=dev(x, (z + j) % NZ, y), device_id_type=MESH,
         ).start()
-    zreq[0, qme] = req2[qme]
+    zreq[:, 0] = req2[:, z]
 
     lanes = lax.broadcasted_iota(I32, (16, 128), 1)
 
     got = pltpu.make_async_remote_copy(
-        src_ref=req2.at[pl.ds(0, NP - 1)], dst_ref=zreq.at[0, pl.ds(0, NP - 1)],
-        send_sem=psem, recv_sem=prsem, device_id=mate, device_id_type=MESH,
+        src_ref=req2.at[:, pl.ds(0, NZ - 1)], dst_ref=zreq.at[:, pl.ds(0, NZ - 1)],
+        send_sem=zsem, recv_sem=zrsem, device_id=mate, device_id_type=MESH,
     )
     got.wait_recv()
 
-    def z_copy(j):
+    def plane_copy(n):
+        tx, ty, q = at_plane(n)
         return pltpu.make_async_remote_copy(
-            src_ref=zreq.at[0], dst_ref=zreq.at[(NZ - j) % NZ],
-            send_sem=zsem.at[j], recv_sem=zrsem.at[(NZ - j) % NZ],
-            device_id=dev(x, (z + j) % NZ, y), device_id_type=MESH,
-        )
-
-    for j in (1, 7, 2, 6, 3, 5, 4):
-        z_copy(j).start()
+            src_ref=zreq.at[q // 8], dst_ref=preq.at[BACK[n]],
+            send_sem=psem.at[n], recv_sem=prsem.at[BACK[n]],
+            device_id=dev(tx, z, ty), device_id_type=MESH,
+        )
+
+    for n in SERVE[1:]:
+        plane_copy(n).start()
+    preq[0] = zreq[qme // 8]
 
     other = pl.multiple_of((1 - c) * FH, 128)
     w_out = []
@@ -134,59 +145,58 @@
 
     c_tab.wait()
 
-    def order(i):
-        return sum(k * (i == n).astype(I32) for n, k in enumerate(ORDER))
-
-    def feature_send(k, m):
-        tx, ty, q = at_plane(m)
-        kk = (NZ - k) % NZ
+    def feature_send(n, j):
+        tx, ty, _ = at_plane(n)
+        back = look(BACK, n)
         return pltpu.make_async_remote_copy(
-            src_ref=stag.at[k * NP + q], dst_ref=xbuf.at[kk * NP + qme],
-            send_sem=fsem.at[k], recv_sem=frsem.at[kk],
-            device_id=dev(tx, (z + k) % NZ, ty), device_id_type=MESH,
-        )
-
-    def gather(k):
-        tz[...] = zreq[k].reshape(NP, 128).T
-        idx = tz[pl.ds(pl.multiple_of(z * 16, 16), 16), :]
-        for q in range(NP):
-            want = jnp.broadcast_to(idx[:, q : q + 1], (16, 128))
+            src_ref=stag.at[n * NZ + j], dst_ref=xbuf.at[back * NZ + (NZ - j) % NZ],
+            send_sem=fsem.at[n // 2], recv_sem=frsem.at[back // 2],
+            device_id=dev(tx, (z + j) % NZ, ty), device_id_type=MESH,
+        )
+
+    def gather(n):
+        tz[...] = preq[n].reshape(NZ, 128).T
+        idx = tz[pl.ds(pl.multiple_of((qme % 8) * 16, 16), 16), :]
+        for j in range(NZ):
+            want = jnp.broadcast_to(idx[:, j : j + 1], (16, 128))
             for t in range(NODE // 128):
-                pick[pl.ds(q * 16, 16), pl.ds(t * 128, 128)] = jnp.where(
+                pick[pl.ds(j * 16, 16), pl.ds(t * 128, 128)] = jnp.where(
                     want == lanes + t * 128, 1.0, 0.0
                 ).astype(BF)
         rows = jnp.dot(pick[...], table_v[...], preferred_element_type=F32)
-        stag[pl.ds(k * NP, NP)] = rows.astype(BF).reshape(NP, ROWS, FH)
+        stag[pl.ds(n * NZ, NZ)] = rows.astype(BF).reshape(NZ, ROWS, FH)
 
     def serve(i, _):
-        k = order(i)
-
-        @pl.when(k > 0)
+        n = look(SERVE, i)
+
+        @pl.when(n > 0)
         def _():
             pltpu.make_async_remote_copy(
-                src_ref=zreq.at[0], dst_ref=zreq.at[k], send_sem=zsem.at[0], recv_sem=zrsem.at[k],
+                src_ref=zreq.at[0], dst_ref=preq.at[n], send_sem=psem.at[0], recv_sem=prsem.at[n],
                 device_id=mate, device_id_type=MESH,
             ).wait_recv()
 
-        gather(k)
-
-        @pl.when(k > 0)
+        gather(n)
+        for j in (4, 3, 5, 2, 6, 1, 7):
+            feature_send(n, j).start()
+
+        @pl.when(n > 0)
         def _():
-            feature_send(k, 0).start()
-
-        for m in range(1, NP):
-            feature_send(k, m).start()
+            feature_send(n, 0).start()
+
         return 0
 
-    lax.fori_loop(0, NZ, serve, 0)
-    xbuf[qme] = stag[qme]
+    lax.fori_loop(0, NP, serve, 0)
+    xbuf[0] = stag[0]
 
     for cp in c_idx:
         cp.wait()
 
     def place(s):
         kk = (((s >> 6) & 7) - z) & 7
-        return (kk << 8) | ((s >> 9) << 6) | (s & 63)
+        m = ((((s >> 9) - x) & 3) << 2) | ((((s >> 4) & 3) - y) & 3)
+        rank = sum(jnp.where(m == a * NY + b, n, 0) for n, (a, b) in enumerate(OFFSET) if n)
+        return (rank << 7) | (kk << 4) | (s & 15)
 
     self_t = place(selfa_v[...]).T
     inv_t = (1.0 / cnta_v[...].astype(F32)).T
@@ -267,10 +277,9 @@
             send_sem=fsem.at[0], recv_sem=frsem.at[k], device_id=mate, device_id_type=MESH,
         ).wait_recv()
 
-    for i in range(NZ):
-        k = (NZ - ORDER[i]) % NZ
-        arrived(k, NP if k else NP - 1)
-        add_up(k, i == 0)
+    for i, p in enumerate(PAIRS):
+        arrived(p, NP if p else NP - 1)
+        add_up(p, i == 0)
 
     for cp in c_bias + c_w:
         cp.wait()
@@ -319,8 +328,8 @@
     out[...] = (s0 * jnp.sqrt(jnp.float32(H)) / jnp.sqrt(squares + H)).astype(BF)
 
     got.wait_send()
-    for j in range(1, NZ):
-        z_copy(j).wait_send()
+    for n in SERVE[1:]:
+        plane_copy(n).wait_send()
     for cp in w_out:
         cp.wait_send()
     for k in range(NZ):
@@ -359,10 +368,12 @@
             pltpu.VMEM((5, SEEDS), I32),
             pltpu.VMEM((SEEDS // 128, 128), I32),
             pltpu.VMEM((SEEDS // 128, 128), I32),
-            pltpu.VMEM((NP, 1, 128), I32),
-            pltpu.VMEM((NZ, NP, 1, 128), I32),
-            pltpu.VMEM((128, NP), I32),
-            pltpu.VMEM((BLK, NODE), BF),
+            pltpu.VMEM((128, 16), I32),
+            pltpu.VMEM((2, NZ, 1, 128), I32),
+            pltpu.VMEM((2, NZ, 1, 128), I32),
+            pltpu.VMEM((NP, NZ, 1, 128), I32),
+            pltpu.VMEM((128, NZ), I32),
+            pltpu.VMEM((128, NODE), BF),
             pltpu.VMEM((NZ * NP, ROWS, FH), BF),
             pltpu.VMEM((NZ * NP, ROWS, FH), BF),
             pltpu.VMEM((2 * HOP, SLOTS), BF),
@@ -381,10 +392,10 @@
             dma((13,)),
             dma((3,)),
             dma((3,)),
+            dma((NP,)),
+            dma((NP,)),
             dma,
             dma,
-            dma((NZ,)),
-            dma((NZ,)),
             dma((NZ,)),
             dma((NZ,)),
             dma((NBLK,)),

time: 63 us -> 62.1 us (0.986)
  the two profiles are of different devices: /device:TPU:71 before, /device:TPU:1 now
where the time goes in v4:
time: 62.1 us; the launch traced here: 62 us
  Pallas kernels  61.3 us (99%)
  local copies, waits for them, and re-layouts  0.66 us (1%)
    pallas_call x1, Pallas kernels, shards(): pl.pallas_call(kernel, name='sage', out_shape=jax.ShapeDtypeStruct((SEEDS...  61.3 us

profile of v4, /device:TPU:1, one launch (start us, length us, event | category | flops | bytes accessed | tf_op | source)
XLA Modules:
  0.0 62.0 jit_solution(16578902776717217870)
XLA Ops:
  0.0 61.3 %sage.1 = bf16[256,256]{1,0:T(8,128)(2,1)S(1)} custom-call(bf16[4096,384]{1,0:T(8,128)(2,1)} %table.1, bf16[1536,256]{1,0:T(8,128)(2,1)} %wa.1, f32[1,512]{1,0:T(1,128)} %bitcast.16, bf16[1024,256]{1,0:T(8,128)(2,1)} %wb.1, f32[1,512]{1,0:T(1,128)} %bitcast.17, s32[16,128]{1,0:T(8,128)} %bitcast.12, s32[10,1024]{1,0:T(8,128)} %bitcast.11, ...), custom_call_target="tpu_custom_call" | custom-call | tf_op jit(solution)/shard_map/sage/pallas_call | solution.py:352
  61.3 0.7 %copy.14 = bf16[256,256]{1,0:T(8,128)(2,1)} copy(bf16[256,256]{1,0:T(8,128)(2,1)S(1)} %sage.1) | data formatting | bytes 262144

commit v5 on v4

--- a/solution.py
+++ b/solution.py
@@ -23,8 +23,8 @@
     (1, 3), (3, 1), (2, 0), (2, 2), (1, 2), (3, 2), (2, 1), (2, 3),
 )
 BACK = tuple(OFFSET.index(((4 - a) % 4, (4 - b) % 4)) for a, b in OFFSET)
-SERVE = (0, 2, 3, 4, 5, 1, 6, 7, 8, 9, 10, 12, 13, 14, 15, 11)
-PAIRS = (1, 2, 0, 3, 4, 6, 7, 5)
+SERVE = (0, 2, 3, 11, 12, 13, 14, 15, 6, 7, 8, 9, 10, 1, 4, 5)
+PAIRS = (1, 6, 7, 3, 4, 5, 0, 2)
 BLK = 256
 NBLK = HOP // BLK
 MESH = pl.DeviceIdType.MESH
@@ -279,7 +279,14 @@
 
     for i, p in enumerate(PAIRS):
         arrived(p, NP if p else NP - 1)
-        add_up(p, i == 0)
+        if i < NZ - 1:
+            add_up(p, i == 0)
+    last = PAIRS[-1]
+    x_last = xbuf[pl.ds(last * NP, NP)].reshape(BLK, FH)
+
+    def finished(lo):
+        at = pl.ds(lo, BLK)
+        return acc[at, :] + jnp.dot(amat[at, pl.ds(last * BLK, BLK)], x_last, preferred_element_type=F32)
 
     for cp in c_bias + c_w:
         cp.wait()
@@ -294,8 +301,8 @@
 
     for b in range(NBLK):
         rows = pl.ds(b * BLK, BLK)
-        own = acc[pl.ds(HOP + b * BLK, BLK), :].astype(BF)
-        mean = (acc[rows, :] * invc[rows, :]).astype(BF)
+        own = finished(HOP + b * BLK).astype(BF)
+        mean = (finished(b * BLK) * invc[rows, :]).astype(BF)
         both = jnp.concatenate([own, mean], axis=1)
         for h in range(2):
             v = jnp.dot(both, wa_v[h], preferred_element_type=F32)

time: 62.1 us -> 59.1 us (0.952)
  Pallas kernels: 61.3 us -> 58.3 us
    pallas_call x1, Pallas kernels: 61.3 us -> 58.3 us  [shards(): pl.pallas_call(kernel, name='sage', out_shape=jax.ShapeDtypeStruct((SEEDS...]
where the time goes in v5:
time: 59.1 us; the launch traced here: 59 us
  Pallas kernels  58.3 us (99%)
  local copies, waits for them, and re-layouts  0.66 us (1%)
    pallas_call x1, Pallas kernels, shards(): pl.pallas_call(kernel, name='sage', out_shape=jax.ShapeDtypeStruct((SEEDS...  58.3 us

profile of v5, /device:TPU:1, one launch (start us, length us, event | category | flops | bytes accessed | tf_op | source)
XLA Modules:
  0.0 59.0 jit_solution(1911345898255260815)
XLA Ops:
  0.0 58.3 %sage.1 = bf16[256,256]{1,0:T(8,128)(2,1)S(1)} custom-call(bf16[4096,384]{1,0:T(8,128)(2,1)} %table.1, bf16[1536,256]{1,0:T(8,128)(2,1)} %wa.1, f32[1,512]{1,0:T(1,128)} %bitcast.16, bf16[1024,256]{1,0:T(8,128)(2,1)} %wb.1, f32[1,512]{1,0:T(1,128)} %bitcast.17, s32[16,128]{1,0:T(8,128)} %bitcast.12, s32[10,1024]{1,0:T(8,128)} %bitcast.11, ...), custom_call_target="tpu_custom_call" | custom-call | tf_op jit(solution)/shard_map/sage/pallas_call | solution.py:359
  58.3 0.7 %copy.14 = bf16[256,256]{1,0:T(8,128)(2,1)} copy(bf16[256,256]{1,0:T(8,128)(2,1)S(1)} %sage.1) | data formatting | bytes 262144

commit v6 on v5

--- a/solution.py
+++ b/solution.py
@@ -26,7 +26,8 @@
 SERVE = (0, 2, 3, 11, 12, 13, 14, 15, 6, 7, 8, 9, 10, 1, 4, 5)
 PAIRS = (1, 6, 7, 3, 4, 5, 0, 2)
 BLK = 256
-NBLK = HOP // BLK
+TAIL = ((0, 384), (384, 384), (768, 128), (896, 128))
+NBLK = len(TAIL)
 MESH = pl.DeviceIdType.MESH
 I32 = jnp.int32
 F32 = jnp.float32
@@ -284,8 +285,8 @@
     last = PAIRS[-1]
     x_last = xbuf[pl.ds(last * NP, NP)].reshape(BLK, FH)
 
-    def finished(lo):
-        at = pl.ds(lo, BLK)
+    def finished(lo, size):
+        at = pl.ds(lo, size)
         return acc[at, :] + jnp.dot(amat[at, pl.ds(last * BLK, BLK)], x_last, preferred_element_type=F32)
 
     for cp in c_bias + c_w:
@@ -295,27 +296,27 @@
 
     def half_copy(b):
         return pltpu.make_async_remote_copy(
-            src_ref=psend.at[b], dst_ref=precv.at[b], send_sem=qsem.at[b], recv_sem=qrsem.at[b],
+            src_ref=psend.at[pl.ds(*TAIL[b])], dst_ref=precv.at[pl.ds(*TAIL[b])], send_sem=qsem.at[b], recv_sem=qrsem.at[b],
             device_id=mate, device_id_type=MESH,
         )
 
-    for b in range(NBLK):
-        rows = pl.ds(b * BLK, BLK)
-        own = finished(HOP + b * BLK).astype(BF)
-        mean = (finished(b * BLK) * invc[rows, :]).astype(BF)
+    for b, (lo, size) in enumerate(TAIL):
+        rows = pl.ds(lo, size)
+        own = finished(HOP + lo, size).astype(BF)
+        mean = (finished(lo, size) * invc[rows, :]).astype(BF)
         both = jnp.concatenate([own, mean], axis=1)
         for h in range(2):
             v = jnp.dot(both, wa_v[h], preferred_element_type=F32)
             part[rows, pl.ds(h * HH, HH)] = v
-            psend[b, :, pl.ds(h * HH, HH)] = v.astype(BF)
+            psend[rows, pl.ds(h * HH, HH)] = v.astype(BF)
         half_copy(b).start()
 
-    for b in range(NBLK):
-        rows = pl.ds(b * BLK, BLK)
+    for b, (lo, size) in enumerate(TAIL):
+        rows = pl.ds(lo, size)
         half_copy(b).wait_recv()
-        v = part[rows, :] + precv[b].astype(F32) + ba_v[...]
+        v = part[rows, :] + precv[rows, :].astype(F32) + ba_v[...]
         hid = jnp.maximum(v, 0.0).astype(BF)
-        tot = jnp.dot(bmat[:, pl.ds(b * BLK, BLK)], hid, preferred_element_type=F32)
+        tot = jnp.dot(bmat[:, rows], hid, preferred_element_type=F32)
         if b == 0:
             accb[...] = tot
         else:
@@ -391,8 +392,8 @@
             pltpu.VMEM((HOP, 1), I32),
             pltpu.VMEM((HOP, 1), F32),
             pltpu.VMEM((HOP, H), F32),
-            pltpu.VMEM((NBLK, BLK, H), BF),
-            pltpu.VMEM((NBLK, BLK, H), BF),
+            pltpu.VMEM((HOP, H), BF),
+            pltpu.VMEM((HOP, H), BF),
             pltpu.VMEM((2 * SEEDS, HOP), BF),
             pltpu.VMEM((2 * SEEDS, H), F32),
             pltpu.VMEM((SEEDS, 1), F32),

time: 59.1 us -> 59.3 us (level)
  no operation moved by 1% of the time
where the time goes in v6:
time: 59.3 us; the launch traced here: 59.1 us
  Pallas kernels  58.5 us (99%)
  local copies, waits for them, and re-layouts  0.66 us (1%)
    pallas_call x1, Pallas kernels, shards(): pl.pallas_call(kernel, name='sage', out_shape=jax.ShapeDtypeStruct((SEEDS...  58.5 us

profile of v6, /device:TPU:1, one launch (start us, length us, event | category | flops | bytes accessed | tf_op | source)
XLA Modules:
  0.0 59.1 jit_solution(2401982886264878962)
XLA Ops:
  0.0 58.5 %sage.1 = bf16[256,256]{1,0:T(8,128)(2,1)S(1)} custom-call(bf16[4096,384]{1,0:T(8,128)(2,1)} %table.1, bf16[1536,256]{1,0:T(8,128)(2,1)} %wa.1, f32[1,512]{1,0:T(1,128)} %bitcast.16, bf16[1024,256]{1,0:T(8,128)(2,1)} %wb.1, f32[1,512]{1,0:T(1,128)} %bitcast.17, s32[16,128]{1,0:T(8,128)} %bitcast.12, s32[10,1024]{1,0:T(8,128)} %bitcast.11, ...), custom_call_target="tpu_custom_call" | custom-call | tf_op jit(solution)/shard_map/sage/pallas_call | solution.py:360
  58.5 0.7 %copy.14 = bf16[256,256]{1,0:T(8,128)(2,1)} copy(bf16[256,256]{1,0:T(8,128)(2,1)S(1)} %sage.1) | data formatting | bytes 262144
